TPU v7x, 512 devices: a whole 4x8x8 slice. The times are simulated.
512 devices in a mesh: dp: 64 (over z, x, core), tensor: 8 (over y).
Axes of the slice: x: 4, y: 8, z: 8, core: 2. Of those that a mesh axis runs over, the one named last changes fastest.
Arguments:
- residual: bfloat16 [16384, 4096], P('dp', 'tensor'), may hold values from -6 to 6
- fresh_qkv: bfloat16 [16384, 3, 2048], P('dp', None, 'tensor'), may hold values from -110 to 110
- active: int32 [16384], P('dp'), may hold values from 0 to 1
- home_slot: int32 [16384], P('dp'), may hold values from 0 to 16383, as said below
- kv_cache: bfloat16 [16384, 2, 16, 2048], P('dp', None, None, 'tensor'), may hold values from -6 to 6
- lengths: int32 [16384], P('dp'), may hold values from 2 to 16
- w_out: bfloat16 [2048, 4096], P('tensor'), may hold values from -0.125 to 0.125
Outputs:
- updated: bfloat16 [16384, 4096], P('dp', 'tensor')
Inputs may be any that keep to these rules, and one draw needn't show every extreme that they name: Each dp group owns the slots 256 * g to 256 * g + 255; home_slot is a permutation. Among the streams of one dp group, at most 4 active streams have slots in the same owning group, and this is reached in every draw.
All inputs are finite; a program needn't handle non-finite values.
Results may differ from a plain program's by a relative error of at most 0.0062.
Values may be sent and summed in bfloat16 or wider, within the bound.
A program may use at most 64 MiB of HBM per device.

v0:
```python
import jax
import jax.numpy as jnp
from jax import lax
from jax.sharding import PartitionSpec as P

HD = 128


def attend_local(fresh_rows, kv_cache, lengths, heads_local):
    streams_here = fresh_rows.shape[0]
    cache_len = kv_cache.shape[2]
    head_size = fresh_rows.shape[1] // (3 * heads_local)
    score_scale = head_size ** (-0.5)
    fresh_split = fresh_rows.reshape(streams_here, 3, heads_local, head_size)
    query = fresh_split[:, 0]
    key_rows = kv_cache[:, 0].reshape(streams_here, cache_len, heads_local, head_size)
    value_rows = kv_cache[:, 1].reshape(streams_here, cache_len, heads_local, head_size)
    scores = (
        jnp.einsum("bhd,blhd->bhl", query, key_rows, preferred_element_type=jnp.float32)
        * score_scale
    )
    positions = jnp.arange(cache_len, dtype=jnp.int32)
    in_cache = positions[None, None, :] < lengths[:, None, None]
    scores = jnp.where(in_cache, scores, jnp.float32(-1e30))
    own_score = (
        jnp.sum(query.astype(jnp.float32) * fresh_split[:, 1].astype(jnp.float32), axis=-1)
        * score_scale
    )
    row_max = jnp.maximum(jnp.max(scores, axis=-1), own_score)
    weights_raw = jnp.exp(scores - row_max[..., None])
    own_raw = jnp.exp(own_score - row_max)
    denominator = jnp.sum(weights_raw, axis=-1) + own_raw
    weights = (weights_raw / denominator[..., None]).astype(jnp.bfloat16)
    own_weight = (own_raw / denominator).astype(jnp.bfloat16)
    mixed = jnp.einsum("bhl,blhd->bhd", weights, value_rows, preferred_element_type=jnp.float32)
    mixed = mixed + own_weight.astype(jnp.float32)[..., None] * fresh_split[:, 2].astype(
        jnp.float32
    )
    return mixed.astype(jnp.bfloat16).reshape(streams_here, heads_local * head_size)


def body(residual, fresh_qkv, active, home_slot, kv_cache, lengths, w_out):
    groups = lax.axis_size("dp")
    group_here = lax.axis_index("dp")
    streams_here = home_slot.shape[0]
    width_here = fresh_qkv.shape[2]
    heads_local = width_here // HD
    capacity = max(2, streams_here // groups)
    slot_count = groups * capacity
    owner_group = home_slot // streams_here
    is_active = active > 0
    earlier = jnp.arange(streams_here)[:, None] < jnp.arange(streams_here)[None, :]
    same_owner = (
        (owner_group[:, None] == owner_group[None, :])
        & is_active[:, None]
        & is_active[None, :]
        & earlier
    )
    send_rank = jnp.sum(same_owner.astype(jnp.int32), axis=0)
    target = owner_group * capacity + send_rank
    placed = (jnp.arange(slot_count, dtype=jnp.int32)[:, None] == target[None, :]) & is_active[
        None, :
    ]
    placing = placed.astype(jnp.bfloat16)
    fresh_flat = fresh_qkv.reshape(streams_here, 3 * width_here)
    send_rows = jnp.dot(placing, fresh_flat, preferred_element_type=jnp.float32).astype(
        jnp.bfloat16
    )
    send_rows = send_rows.reshape(groups, capacity, 3 * width_here)
    slot_ids = jnp.sum(jnp.where(placed, home_slot[None, :] + 1, 0), axis=1) - 1
    slot_ids = slot_ids.reshape(groups, capacity)
    got_rows, got_ids = (
        lax.all_to_all(send_rows, "dp", split_axis=0, concat_axis=0, tiled=True),
        lax.all_to_all(slot_ids, "dp", split_axis=0, concat_axis=0, tiled=True),
    )
    local_slot = got_ids.reshape(slot_count) - group_here * streams_here
    matched = (local_slot[None, :] == jnp.arange(streams_here, dtype=jnp.int32)[:, None]).astype(
        jnp.bfloat16
    )
    owned = jnp.dot(
        matched, got_rows.reshape(slot_count, 3 * width_here), preferred_element_type=jnp.float32
    ).astype(jnp.bfloat16)
    attended = attend_local(owned, kv_cache, lengths, heads_local)
    heads_rows = jnp.dot(matched.T, attended, preferred_element_type=jnp.float32).astype(
        jnp.bfloat16
    )
    returned = lax.all_to_all(
        heads_rows.reshape(groups, capacity, width_here),
        "dp",
        split_axis=0,
        concat_axis=0,
        tiled=True,
    )
    source_rows = jnp.dot(
        placing.T, returned.reshape(slot_count, width_here), preferred_element_type=jnp.float32
    ).astype(jnp.bfloat16)
    partial_rows = jnp.dot(source_rows, w_out, preferred_element_type=jnp.float32)
    gained = lax.psum_scatter(
        partial_rows.astype(jnp.bfloat16), "tensor", scatter_dimension=1, tiled=True
    ).astype(jnp.float32)
    return (residual.astype(jnp.float32) + gained).astype(jnp.bfloat16)


def solution(mesh):
    placed = (
        P("dp", "tensor"),
        P("dp", None, "tensor"),
        P("dp"),
        P("dp"),
        P("dp", None, None, "tensor"),
        P("dp"),
        P("tensor", None),
    )
    return jax.shard_map(
        body, mesh=mesh, in_specs=placed, out_specs=P("dp", "tensor"), check_vma=False
    )
```

profile of v0, /device:TPU:2, one launch (start us, length us, event | category | flops | bytes accessed | tf_op | source)
XLA Modules:
  0.0 129.4 jit_solution(15604849099110428578)
XLA Ops:
  6.5 0.0 copy-start
  6.5 0.8 broadcast_add_fusion.1
  7.4 0.7 broadcast_compare_fusion
  8.1 0.2 convert_reduce_fusion
  8.2 0.1 select_reduce_fusion
  8.4 0.7 sub.45
  9.1 13.9 %all-to-all-start = ((s32[64,1,4]{2,1,0:T(1,128)}), s32[64,1,4]{2,1,0:T(1,128)S(1)}, u32[]{:S(2)}, u32[]{:S(2)}) async-start(s32[64,1,4]{2,1,0:T(1,128)} %bitcast), calls=%async_computation | async-start | bytes 65536 | tf_op jit(solution)/shard_map/all_to_all | solution.py:74
  23.0 1.2 copy.19
  24.1 0.3 convolution_convert_fusion.2
  24.4 0.9 reshape.103
  25.3 6.2 %all-to-all-done = s32[64,1,4]{2,1,0:T(1,128)S(1)} async-done(((s32[64,1,4]{2,1,0:T(1,128)}), s32[64,1,4]{2,1,0:T(1,128)S(1)}, u32[]{:S(2)}, u32[]{:S(2)}) %all-to-all-start) | async-done | bytes 1056 | tf_op jit(solution)/shard_map/all_to_all | solution.py:74
  31.5 5.5 %all-to-all-start.1 = ((bf16[64,4,768]{2,1,0:T(4,128)(2,1)}), bf16[64,4,768]{2,1,0:T(4,128)(2,1)S(1)}, u32[]{:S(2)}, u32[]{:S(2)}) async-start(bf16[64,4,768]{2,1,0:T(4,128)(2,1)} %reshape.103), calls=%async_computation.1 | async-start | bytes 786432 | tf_op jit(solution)/shard_map/all_to_all | solution.py:73
  37.0 0.0 reduce-scatter.2.cloned.1.call-start
  37.1 4.6 %fusion.29 = (bf16[256,1,16,256]{3,2,1,0:T(8,128)(2,1)}, bf16[256,1,16,256]{3,2,1,0:T(8,128)(2,1)}) fusion(bf16[256,2,16,256]{3,2,1,0:T(8,128)(2,1)} %param.11), kind=kLoop, calls=%fused_computation.56 | loop fusion | bytes 8388608 | tf_op jit(solution)/shard_map/slice | solution.py:17
  41.7 4.0 %reshape_squeeze.6 = bf16[256,16,2,128]{3,2,1,0:T(2,128)(2,1)} reshape(bf16[256,1,16,256]{3,2,1,0:T(8,128)(2,1)} %get-tuple-element.6) | data formatting | bytes 4194304 | tf_op jit(solution)/shard_map/reshape;squeeze | solution.py:16
  45.7 0.0 copy-start.2
  45.7 4.0 %reshape_squeeze.7 = bf16[256,16,2,128]{3,2,1,0:T(2,128)(2,1)} reshape(bf16[256,1,16,256]{3,2,1,0:T(8,128)(2,1)} %get-tuple-element.5) | data formatting | bytes 4194304 | tf_op jit(solution)/shard_map/reshape;squeeze | solution.py:17
  49.6 0.0 copy-done.2
  49.7 0.1 subtract_reduce_fusion
  49.8 0.1 sub.48
  49.9 2.0 %all-to-all-done.1 = bf16[64,4,768]{2,1,0:T(4,128)(2,1)S(1)} async-done(((bf16[64,4,768]{2,1,0:T(4,128)(2,1)}), bf16[64,4,768]{2,1,0:T(4,128)(2,1)S(1)}, u32[]{:S(2)}, u32[]{:S(2)}) %all-to-all-start.1) | async-done | bytes 393248 | tf_op jit(solution)/shard_map/all_to_all | solution.py:73
  51.9 0.1 reshape.104
  52.0 0.3 convolution_convert_fusion.1
  52.2 0.1 reshape.105
  52.3 0.3 fusion.6
  52.7 0.1 slice_bitcast_fusion.2
  52.8 0.1 copy.22
  52.9 2.8 %fusion.2 = f32[256,2,1,16]{3,2,1,0:T(1,128)S(1)} fusion(bf16[256,16,2,128]{3,2,1,0:T(2,128)(2,1)} %reshape_squeeze.6, bf16[256,2,128,1]{2,1,0,3:T(2,128)(2,1)S(1)} %slice_bitcast_fusion.2), kind=kOutput, calls=%fused_computation.3 | convolution fusion | flops 2097152 | bytes 2260992 | tf_op jit(solution)/shard_map/bhd,blhd->bhl/dot_general | solution.py:19
  55.7 0.1 copy.26
  55.9 0.2 copy.27
  56.1 0.1 copy.23
  56.2 2.3 %fusion = f32[256,2,1,128]{3,2,1,0:T(1,128)S(1)} fusion(bf16[256,2,16,1]{2,3,1,0:T(2,128)(2,1)S(1)} %copy.27, bf16[256,16,2,128]{3,2,1,0:T(2,128)(2,1)} %reshape_squeeze.7), kind=kOutput, calls=%fused_computation.1 | convolution fusion | flops 2097152 | bytes 2375680 | tf_op jit(solution)/shard_map/bhl,blhd->bhd/dot_general | solution.py:35
  58.5 0.3 fusion.5
  58.9 0.3 convolution_convert_fusion.4
  59.2 18.1 %all_to_all.16 = bf16[64,4,256]{2,1,0:T(4,128)(2,1)S(1)} all-to-all(bf16[64,4,256]{2,1,0:T(4,128)(2,1)S(1)} %reshape.107), channel_id=1, replica_groups=mesh['dp'=64,'tensor'=8] {'dp'}, dimensions={0} | all-to-all | bytes 262144 | tf_op jit(solution)/shard_map/all_to_all | solution.py:87
  77.3 0.0 copy-done
  77.3 2.2 %convolution_convert_fusion = bf16[256,4096]{1,0:T(8,128)(2,1)} fusion(bf16[256,4096]{1,0:T(8,128)(2,1)S(1)} %copy-done, bf16[256,256]{1,0:T(8,128)(2,1)S(1)} %reshape.108, s32[256]{0:T(256)S(1)} %multiply_add_fusion, pred[256]{0:T(512)(128)(4,1)S(1)} %broadcast_compare_fusion), kind=kOutput, calls=%fused_computation | convolution fusion | flops 571670528 | bytes 4326656 | tf_op jit(solution)/shard_map/dot_general | solution.py:97
  79.6 0.0 copy-start.1
  79.6 0.0 reduce-scatter.2.cloned.1.call-update
  79.6 41.3 %reduce-scatter.2.cloned.1.call-done = bf16[256,512]{1,0:T(8,128)(2,1)} async-done(((bf16[256,4096]{1,0:T(8,128)(2,1)}), bf16[256,512]{1,0:T(8,128)(2,1)}) %reduce-scatter.2.cloned.1.call-update) | async-done | bytes 262160 | tf_op jit(solution)/shard_map/reduce_scatter | solution.py:98
  120.8 0.0 copy-done.1
  120.8 1.7 %add_convert_fusion = bf16[256,512]{1,0:T(8,128)(2,1)} fusion(bf16[256,512]{1,0:T(8,128)(2,1)} %reduce-scatter.2.cloned.1.call-done, bf16[256,512]{1,0:T(8,128)(2,1)S(1)} %copy-done.1), kind=kLoop, calls=%fused_computation.9 | loop fusion | flops 524288 | bytes 786432 | tf_op jit(solution)/shard_map/convert_element_type | solution.py:101
  (10 shorter events, 0.2 us)
Async XLA Ops:
  6.5 70.8 %copy-start = (bf16[256,4096]{1,0:T(8,128)(2,1)S(1)}, bf16[256,4096]{1,0:T(8,128)(2,1)}, u32[]{:S(2)}) copy-start(bf16[256,4096]{1,0:T(8,128)(2,1)} %param.13) | copy-start | bytes 6291460
  9.1 22.4 %all-to-all-start = ((s32[64,1,4]{2,1,0:T(1,128)}), s32[64,1,4]{2,1,0:T(1,128)S(1)}, u32[]{:S(2)}, u32[]{:S(2)}) async-start(s32[64,1,4]{2,1,0:T(1,128)} %bitcast), calls=%async_computation | async-start | bytes 65536 | tf_op jit(solution)/shard_map/all_to_all | solution.py:74
  31.5 20.4 %all-to-all-start.1 = ((bf16[64,4,768]{2,1,0:T(4,128)(2,1)}), bf16[64,4,768]{2,1,0:T(4,128)(2,1)S(1)}, u32[]{:S(2)}, u32[]{:S(2)}) async-start(bf16[64,4,768]{2,1,0:T(4,128)(2,1)} %reshape.103), calls=%async_computation.1 | async-start | bytes 786432 | tf_op jit(solution)/shard_map/all_to_all | solution.py:73
  37.0 83.8 %reduce-scatter.2.cloned.1.call-start = ((), (), s32[]{:S(2)}) async-start(), calls=%async_computation.4 | async-start | bytes 2359296 | tf_op jit(solution)/shard_map/reduce_scatter | solution.py:98
  45.7 4.0 %copy-start.2 = (s32[256]{0:T(256)S(1)}, s32[256]{0:T(256)}, u32[]{:S(2)}) copy-start(s32[256]{0:T(256)} %param.12) | copy-start | bytes 3076
  79.6 41.3 %copy-start.1 = (bf16[256,512]{1,0:T(8,128)(2,1)S(1)}, bf16[256,512]{1,0:T(8,128)(2,1)}, u32[]{:S(2)}) copy-start(bf16[256,512]{1,0:T(8,128)(2,1)} %param.7) | copy-start | bytes 786436
Sparse Core Ops, SparseCore 0:
  79.7 41.0 reduce-scatter.1
where the time goes:
time: 130 us; the launch traced here: 129 us
  waiting for transfers between devices  49.5 us (38%)
  starting transfers between devices  19.4 us (15%)
  blocking collectives  18.1 us (14%)
  local copies, waits for them, and re-layouts  16.2 us (12%)
  between operations  13.6 us (10%)
  matrix products  8.11 us (6%)
  other arithmetic  4.43 us (3%)
    reduce_scatter x1, waiting for transfers between devices, body(): lax.psum_scatter(partial_rows.astype(jnp.bfloat16), 'tensor', scatter_dim...  41.3 us
    all_to_all x1, blocking collectives, body(): lax.all_to_all(heads_rows.reshape(groups, capacity, width_here), 'dp', sp...  18.1 us
    all_to_all x1, starting transfers between devices, body(): lax.all_to_all(slot_ids, 'dp', split_axis=0, concat_axis=0, tiled=True)  13.9 us
    all_to_all x1, waiting for transfers between devices, body(): lax.all_to_all(slot_ids, 'dp', split_axis=0, concat_axis=0, tiled=True)  6.2 us
    all_to_all x1, starting transfers between devices, body(): lax.all_to_all(send_rows, 'dp', split_axis=0, concat_axis=0, tiled=True)  5.52 us
    slice x1, local copies, waits for them, and re-layouts, attend_local(): kv_cache[:, 1].reshape(streams_here, cache_len, heads_local, head_size)  4.58 us
    another operation x1, local copies, waits for them, and re-layouts, attend_local(): kv_cache[:, 1].reshape(streams_here, cache_len, heads_local, head_size)  3.98 us
    another operation x1, local copies, waits for them, and re-layouts, attend_local(): kv_cache[:, 0].reshape(streams_here, cache_len, heads_local, head_size)  3.97 us
  transfers between devices with their start and end apart: 3, of which 3 were waited for; matrix products, arithmetic and copies ran while one was open for 12% of the time, Pallas kernels for 0%

commit v1 on v0

v1 whole, which is shorter than its diff:
```python
import functools

import jax
import jax.numpy as jnp
from jax import lax
from jax.experimental import pallas as pl
from jax.experimental.pallas import tpu as pltpu
from jax.sharding import PartitionSpec as P

MESH = pl.DeviceIdType.MESH
HD = 128
CAP = 4
F32, BF16, I32 = jnp.float32, jnp.bfloat16, jnp.int32


def dot(a, b, ca=1, cb=0):
    return lax.dot_general(a, b, (((ca,), (cb,)), ((), ())), preferred_element_type=F32)


def kernel(
    groups, ring,
    fresh_hbm, act_ref, home_ref, len_ref, kv_hbm, w_hbm, res_hbm,
    out_ref,
    fresh, kv, wcol, res, ids_s, ids_r, send, recv, rsend, rrecv, gath, place, match, owned, score, att, acc,
    lsem, ids_ss, ids_rs, dat_ss, dat_rs, ret_ss, ret_rs,
    wy_s, wy_r, wc_s, wc_r, wx_s, wx_r, wz_s, wz_r, agr_s, agr_r, agl_s, agl_r,
):
    n = act_ref.shape[1]
    length = kv.shape[2]
    cols = wcol.shape[2]
    depth = wcol.shape[1]
    me = lax.axis_index("dp")
    y = lax.axis_index("tensor")
    core = lax.rem(me, 2)
    xbit = lax.rem(me // 2, 2)
    partner = me + 1 - 2 * core
    across = me + 2 - 4 * xbit
    quarter = depth // 4

    def dp_peer(k):
        return lax.rem(me + k, groups)

    def y_peer(d):
        return lax.rem(y + d, ring)

    fresh_cp = pltpu.make_async_copy(fresh_hbm, fresh, lsem.at[0])
    fresh_cp.start()

    barrier = pltpu.get_barrier_semaphore()

    def greet(k, c):
        pl.semaphore_signal(barrier, inc=1, device_id={"dp": dp_peer(k)}, device_id_type=MESH)
        return c

    lax.fori_loop(1, groups, greet, 0)
    for d in range(1, ring):
        pl.semaphore_signal(barrier, inc=1, device_id={"tensor": y_peer(d)}, device_id_type=MESH)

    kv_cp = pltpu.make_async_copy(kv_hbm, kv, lsem.at[1])
    kv_cp.start()
    wown_cp = pltpu.make_async_copy(
        w_hbm.at[:, pl.ds(pl.multiple_of(y * cols, cols), cols)], wcol.at[y], lsem.at[2])
    wown_cp.start()
    res_cp = pltpu.make_async_copy(res_hbm, res, lsem.at[3])
    res_cp.start()

    home = home_ref[...]
    active = act_ref[...] > 0
    owner = home // n
    local_id = (home - owner * n + 1).astype(F32)
    of_group = (owner == lax.broadcasted_iota(I32, (groups, n), 0)) & active
    one_hot = jnp.where(of_group, 1.0, 0.0).astype(F32)
    before = jnp.where(
        lax.broadcasted_iota(I32, (n, n), 0) < lax.broadcasted_iota(I32, (n, n), 1), 1.0, 0.0
    ).astype(BF16)
    earlier = dot(one_hot.astype(BF16), before)
    rank = jnp.sum(one_hot * earlier, axis=0, keepdims=True)
    lane = lax.broadcasted_iota(I32, (groups, 128), 1)
    mine = (lane // 8) == lax.rem(me, 16)
    id_rows = jnp.zeros((groups, 128), F32)
    for r in range(CAP):
        value = jnp.sum(jnp.where(rank == r, one_hot * local_id, 0.0), axis=1, keepdims=True)
        id_rows = jnp.where(mine & (lane % 4 == r), value, id_rows)
    ids_s[...] = id_rows.reshape(groups, 1, 128)
    target = jnp.where(active, owner * 8 + rank.astype(I32), -64)
    spot = lax.broadcasted_iota(I32, (groups * 8, n), 0)
    for h in range(2):
        place[h] = jnp.where(spot == target + 4 * h, 1.0, 0.0).astype(BF16)
    fresh_cp.wait()
    for k in range(3):
        rows = dot(place[0], fresh[k, :, 0:HD]) + dot(place[1], fresh[k, :, HD:2 * HD])
        send[:, :, k * HD:(k + 1) * HD] = rows.astype(BF16).reshape(groups, 8, HD)

    pl.semaphore_wait(barrier, groups - 1 + ring - 1)

    def ids_copy(k):
        to = dp_peer(k)
        return pltpu.make_async_remote_copy(
            ids_s.at[to], ids_r.at[me], ids_ss, ids_rs, device_id={"dp": to}, device_id_type=MESH)

    def dat_copy(k):
        to = dp_peer(k)
        return pltpu.make_async_remote_copy(
            send.at[to], recv.at[me], dat_ss, dat_rs, device_id={"dp": to}, device_id_type=MESH)

    def ret_copy(k):
        to = dp_peer(k)
        return pltpu.make_async_remote_copy(
            rsend.at[to], rrecv.at[me], ret_ss, ret_rs, device_id={"dp": to}, device_id_type=MESH)

    def whole(src, dst, ss, rs):
        return pltpu.make_async_remote_copy(
            src.at[pl.ds(0, groups - 1)], dst.at[pl.ds(0, groups - 1)], ss, rs,
            device_id={"dp": partner}, device_id_type=MESH)

    def go(k, c):
        ids_copy(k).start()
        dat_copy(k).start()
        return c

    lax.fori_loop(1, groups, go, 0)
    own_ids = pltpu.make_async_copy(ids_s.at[me], ids_r.at[me], lsem.at[4])
    own_ids.start()
    own_dat = pltpu.make_async_copy(send.at[me], recv.at[me], lsem.at[5])
    own_dat.start()

    def part(cbit, xb):
        return pl.ds(pl.multiple_of((xb * 2 + cbit) * quarter, quarter), quarter)

    mypart = part(core, xbit)
    otherpart = part(core, 1 - xbit)
    order = [1, 7, 2, 6, 3, 5, 4]

    def wy_copy(d):
        to = y_peer(d)
        return pltpu.make_async_remote_copy(
            w_hbm.at[mypart, pl.ds(pl.multiple_of(to * cols, cols), cols)], wcol.at[y, mypart],
            wy_s.at[d], wy_r.at[d], device_id={"tensor": to}, device_id_type=MESH)

    def fwd_copy(d, rows, ss, rs, to):
        src = lax.rem(y + ring - d, ring)
        return pltpu.make_async_remote_copy(
            wcol.at[src, rows], wcol.at[src, rows], ss.at[d], rs.at[d],
            device_id={"dp": to}, device_id_type=MESH)

    def wc_copy(d):
        return fwd_copy(d, mypart, wc_s, wc_r, partner)

    def wx_copy(d):
        return fwd_copy(d, mypart, wx_s, wx_r, across)

    def wz_copy(d):
        return fwd_copy(d, otherpart, wz_s, wz_r, partner)

    for d in order:
        wy_copy(d).start()

    def pass_on(d):
        wy_copy(d).wait_recv()
        wx_copy(d).start()
        wc_copy(d).start()

    def pass_twice(d):
        wx_copy(d).wait_recv()
        wz_copy(d).start()

    for d in order[:4]:
        pass_on(d)

    own_ids.wait()
    own_dat.wait()
    whole(ids_s, ids_r, ids_ss, ids_rs).wait_recv()
    slot = lax.broadcasted_iota(I32, (n, 128), 0) + 1
    half = (lax.broadcasted_iota(I32, (n, 128), 1) % 8) // 4
    for b in range(groups // 16):
        ids = ids_r[16 * b]
        for i in range(1, 16):
            ids = ids + ids_r[16 * b + i]
        hit = ids.astype(I32) == slot
        for h in range(2):
            match[h, :, b * 128:(b + 1) * 128] = jnp.where(hit & (half == h), 1.0, 0.0).astype(BF16)
    len_row = len_ref[...]
    eye = lax.broadcasted_iota(I32, (n, n), 0) == lax.broadcasted_iota(I32, (n, n), 1)
    lengths = dot(jnp.where(eye, len_row, 0).astype(BF16), jnp.ones((n, 16 * length), BF16))
    whole(send, recv, dat_ss, dat_rs).wait_recv()
    for k in range(3):
        rows = recv[:, :, k * HD:(k + 1) * HD].reshape(groups * 8, HD)
        for h in range(2):
            owned[h, :, k * HD:(k + 1) * HD] = dot(match[h], rows).astype(BF16)

    kv_cp.wait()
    blocks = n // 16
    for h in range(2):
        cl = pl.ds(h * HD, HD)
        for i in range(blocks):
            keys = kv[16 * i:16 * i + 16, 0, :, cl].reshape(16 * length, HD)
            score[16 * i:16 * i + 16] = dot(owned[h, 16 * i:16 * i + 16, 0:HD], keys, 1, 1)
        scale = HD ** -0.5
        lane_i = lax.broadcasted_iota(I32, (n, 16 * length), 1)
        row_i = lax.broadcasted_iota(I32, (n, 16 * length), 0)
        valid = (lane_i // length == row_i % 16) & ((lane_i % length).astype(F32) < lengths)
        s = jnp.where(valid, score[...] * scale, -1e30)
        q = owned[h, :, 0:HD].astype(F32)
        own = jnp.sum(q * owned[h, :, HD:2 * HD].astype(F32), axis=1, keepdims=True) * scale
        top = jnp.maximum(jnp.max(s, axis=1, keepdims=True), own)
        e = jnp.where(valid, jnp.exp(s - top), 0.0)
        own_e = jnp.exp(own - top)
        z = jnp.sum(e, axis=1, keepdims=True) + own_e
        w = (e / z).astype(BF16)
        own_w = (own_e / z).astype(BF16).astype(F32)
        for i in range(blocks):
            values = kv[16 * i:16 * i + 16, 1, :, cl].reshape(16 * length, HD)
            mixed = dot(w[16 * i:16 * i + 16], values)
            fresh_v = owned[h, 16 * i:16 * i + 16, 2 * HD:3 * HD].astype(F32)
            mixed = mixed + own_w[16 * i:16 * i + 16] * fresh_v
            att[h, 16 * i:16 * i + 16] = mixed.astype(BF16)
    back = dot(match[0], att[0], 0, 0) + dot(match[1], att[1], 0, 0)
    rsend[...] = back.astype(BF16).reshape(groups, 8, HD)

    def go_back(k, c):
        ret_copy(k).start()
        return c

    lax.fori_loop(1, groups, go_back, 0)
    own_ret = pltpu.make_async_copy(rsend.at[me], rrecv.at[me], lsem.at[6])
    own_ret.start()

    for d in order[4:]:
        pass_on(d)
    for d in order:
        pass_twice(d)

    own_ret.wait()
    whole(rsend, rrecv, ret_ss, ret_rs).wait_recv()
    back_rows = rrecv[...].reshape(groups * 8, HD)
    for h in range(2):
        gath[y, :, h * HD:(h + 1) * HD] = dot(place[h], back_rows, 0, 0).astype(BF16)

    hr = n // 2

    def ring_copy(s, hf, way):
        src = lax.rem(y + (ring - s if way > 0 else s), ring)
        to = lax.rem(y + (1 if way > 0 else ring - 1), ring)
        ss, rs = (agr_s, agr_r) if way > 0 else (agl_s, agl_r)
        piece = gath.at[src, pl.ds(hf * hr, hr)]
        return pltpu.make_async_remote_copy(
            piece, piece, ss.at[2 * s + hf], rs.at[2 * s + hf],
            device_id={"tensor": to}, device_id_type=MESH)

    last = ring // 2 - 1
    moves = [(s, hf, way) for s in range(last + 1) for hf, way in ((0, 1), (1, -1), (1, 1), (0, -1))
             if s < last or (hf == 0) == (way > 0)]
    for m in moves:
        if m[0] == 0:
            ring_copy(*m).start()

    for d in order:
        wc_copy(d).wait_recv()
        wz_copy(d).wait_recv()
    wown_cp.wait()
    res_cp.wait()

    acc[...] = res[...].astype(F32) + dot(gath[y], wcol[y])
    for s in range(last + 1):
        for m in moves:
            if m[0] == s:
                ring_copy(*m).wait_recv()
                nxt = (s + 1, m[1], m[2])
                if nxt in moves:
                    ring_copy(*nxt).start()
        right = lax.rem(y + ring - s - 1, ring)
        left = lax.rem(y + s + 1, ring)
        if s < last:
            acc[...] += dot(gath[right], wcol[right]) + dot(gath[left], wcol[left])
        else:
            out_ref[...] = (acc[...] + dot(gath[right], wcol[right])).astype(BF16)

    whole(ids_s, ids_r, ids_ss, ids_rs).wait_send()
    whole(send, recv, dat_ss, dat_rs).wait_send()
    whole(rsend, rrecv, ret_ss, ret_rs).wait_send()
    for d in order:
        wy_copy(d).wait_send()
        wc_copy(d).wait_send()
        wx_copy(d).wait_send()
        wz_copy(d).wait_send()
    for m in moves:
        ring_copy(*m).wait_send()


def body(groups, ring, residual, fresh_qkv, active, home_slot, kv_cache, lengths, w_out):
    n = home_slot.shape[0]
    width = fresh_qkv.shape[2]
    cols = residual.shape[1]
    depth = w_out.shape[0]
    length = kv_cache.shape[2]
    hbm = pl.BlockSpec(memory_space=pl.ANY)
    vm = pl.BlockSpec(memory_space=pltpu.VMEM)
    dma = pltpu.SemaphoreType.DMA
    return pl.pallas_call(
        functools.partial(kernel, groups, ring),
        out_shape=jax.ShapeDtypeStruct((n, cols), BF16),
        in_specs=[hbm, vm, vm, vm, hbm, hbm, hbm],
        out_specs=vm,
        scratch_shapes=[
            pltpu.VMEM((3, n, width), BF16),
            pltpu.VMEM(kv_cache.shape, BF16),
            pltpu.VMEM((ring, depth, cols), BF16),
            pltpu.VMEM((n, cols), BF16),
            pltpu.VMEM((groups, 1, 128), F32),
            pltpu.VMEM((groups, 1, 128), F32),
            pltpu.VMEM((groups, 8, 3 * HD), BF16),
            pltpu.VMEM((groups, 8, 3 * HD), BF16),
            pltpu.VMEM((groups, 8, HD), BF16),
            pltpu.VMEM((groups, 8, HD), BF16),
            pltpu.VMEM((ring, n, width), BF16),
            pltpu.VMEM((2, groups * 8, n), BF16),
            pltpu.VMEM((2, n, groups * 8), BF16),
            pltpu.VMEM((2, n, 3 * HD), BF16),
            pltpu.VMEM((n, 16 * length), F32),
            pltpu.VMEM((2, n, HD), BF16),
            pltpu.VMEM((n, cols), F32),
            dma((7,)),
            dma, dma, dma, dma, dma, dma,
            dma((ring,)), dma((ring,)), dma((ring,)), dma((ring,)),
            dma((ring,)), dma((ring,)), dma((ring,)), dma((ring,)),
            dma((ring,)), dma((ring,)), dma((ring,)), dma((ring,)),
        ],
        compiler_params=pltpu.CompilerParams(collective_id=0, has_side_effects=True),
    )(
        fresh_qkv.transpose(1, 0, 2), active.reshape(1, n), home_slot.reshape(1, n), lengths.reshape(1, n),
        kv_cache, w_out, residual,
    )


def solution(mesh):
    placed = (
        P("dp", "tensor"),
        P("dp", None, "tensor"),
        P("dp"),
        P("dp"),
        P("dp", None, None, "tensor"),
        P("dp"),
        P("tensor", None),
    )
    return jax.shard_map(
        functools.partial(body, mesh.shape["dp"], mesh.shape["tensor"]),
        mesh=mesh, in_specs=placed, out_specs=P("dp", "tensor"), check_vma=False,
    )
```

time: 130 us -> 58.7 us (0.45)
  the two profiles are of different devices: /device:TPU:2 before, /device:TPU:4 now
where the time goes in v1:
time: 58.7 us; the launch traced here: 58.6 us
  Pallas kernels  56.9 us (97%)
  local copies, waits for them, and re-layouts  1.67 us (3%)
    pallas_call x1, Pallas kernels, body(): pl.pallas_call(functools.partial(kernel, groups, ring), out_shape=jax.Sha...  56.9 us
    unnamed x1, local copies, waits for them, and re-layouts  1.67 us

profile of v1, /device:TPU:4, one launch (start us, length us, event | category | flops | bytes accessed | tf_op | source)
XLA Modules:
  0.0 58.6 jit_solution(1205201640502995809)
XLA Ops:
  0.0 56.9 %shard_map.73 = bf16[256,512]{1,0:T(8,128)(2,1)} custom-call(bf16[3,256,256]{2,1,0:T(8,128)(2,1)} %bitcast.4, s32[1,256]{1,0:T(1,128)} %bitcast.5, s32[1,256]{1,0:T(1,128)} %bitcast.6, s32[1,256]{1,0:T(1,128)} %bitcast.7, bf16[256,2,16,256]{3,2,1,0:T(8,128)(2,1)} %kv_hbm.1, bf16[256,4096]{1,0:T(8,128)(2,1)} %w_hbm.1, bf16[256,512]{1,0:T(8,128)(2,1)} %res_hbm.1), custom_call_target="tpu_custom_call" | custom-call | tf_op jit(solution)/shard_map/pallas_call | solution.py:299
  56.9 1.7 %copy.9 = bf16[256,512]{1,0:T(8,128)(2,1)} copy(bf16[256,512]{1,0:T(8,128)(2,1)} %shard_map.73) | data formatting | bytes 524288

commit v2 on v1

v2 whole, which is shorter than its diff:
```python
import functools

import jax
import jax.numpy as jnp
from jax import lax
from jax.experimental import pallas as pl
from jax.experimental.pallas import tpu as pltpu
from jax.sharding import PartitionSpec as P

MESH = pl.DeviceIdType.MESH
HD = 128
CAP = 4
F32, BF16, I32 = jnp.float32, jnp.bfloat16, jnp.int32


def dot(a, b, ca=1, cb=0):
    return lax.dot_general(a, b, (((ca,), (cb,)), ((), ())), preferred_element_type=F32)


def kernel(
    groups, ring,
    fresh_hbm, act_hbm, home_hbm, len_hbm, kv_hbm, w_hbm, res_hbm,
    out_ref,
    fresh, act_ref, home_ref, len_ref, kv, wcol, res, ids_s, ids_r, send, recv, rsend, rrecv, lse_s, lse_r,
    gath, place, match, owned, score, att, own_sc, live, acc,
    lsem, ids_ss, ids_rs, dat_ss, dat_rs, lse_ss, lse_rs, ret_ss, ret_rs, wy_s, wy_r, wm_s, wm_r, ag_s, ag_r,
):
    n = act_ref.shape[1]
    length = kv.shape[2]
    cols = wcol.shape[2]
    depth = wcol.shape[1]
    planes = groups // 8
    me = lax.axis_index("dp")
    y = lax.axis_index("tensor")
    z, x, core = me // 8, lax.rem(me, 8) // 2, lax.rem(me, 2)
    partner = me + 1 - 2 * core

    beside = [lax.rem(me + m, 8) for m in range(8)]

    def each_peer(act):
        def plane(i, c):
            dz = planes // 2 + (1 - 2 * lax.rem(i, 2)) * ((i + 1) // 2)
            base = lax.rem(z + dz, planes) * 8
            for m in range(8):
                act(base + beside[7 - m])
            return c

        lax.fori_loop(0, planes - 1, plane, 0)
        for m in range(7):
            act(z * 8 + beside[7 - m])

    def y_peer(d):
        return lax.rem(y + d, ring)

    barrier = pltpu.get_barrier_semaphore()

    def greet(to):
        pl.semaphore_signal(barrier, inc=1, device_id={"dp": to}, device_id_type=MESH)

    small = [pltpu.make_async_copy(a, b, lsem.at[i]) for i, (a, b) in enumerate(
        ((home_hbm, home_ref), (act_hbm, act_ref), (len_hbm, len_ref)))]
    for cp in small:
        cp.start()
    fresh_cp = pltpu.make_async_copy(fresh_hbm, fresh, lsem.at[3])
    fresh_cp.start()
    each_peer(greet)
    for d in range(1, ring):
        pl.semaphore_signal(barrier, inc=1, device_id={"tensor": y_peer(d)}, device_id_type=MESH)
    kv_cp = pltpu.make_async_copy(kv_hbm, kv, lsem.at[4])
    kv_cp.start()
    wown_cp = pltpu.make_async_copy(
        w_hbm.at[:, pl.ds(pl.multiple_of(y * cols, cols), cols)], wcol.at[ring - 1], lsem.at[5])
    wown_cp.start()
    res_cp = pltpu.make_async_copy(res_hbm, res, lsem.at[6])
    res_cp.start()

    for cp in small:
        cp.wait()
    home = home_ref[...]
    active = act_ref[...] > 0
    owner = home // n
    local_id = (home - owner * n + 1).astype(F32)
    of_group = (owner == lax.broadcasted_iota(I32, (groups, n), 0)) & active
    one_hot = jnp.where(of_group, 1.0, 0.0).astype(F32)
    before = jnp.where(
        lax.broadcasted_iota(I32, (n, n), 0) < lax.broadcasted_iota(I32, (n, n), 1), 1.0, 0.0
    ).astype(BF16)
    earlier = dot(one_hot.astype(BF16), before)
    rank = jnp.sum(one_hot * earlier, axis=0, keepdims=True)
    lane = lax.broadcasted_iota(I32, (groups, 128), 1)
    mine = (lane // 8) == lax.rem(me, 16)
    id_rows = jnp.zeros((groups, 128), F32)
    for r in range(CAP):
        value = jnp.sum(jnp.where(rank == r, one_hot * local_id, 0.0), axis=1, keepdims=True)
        id_rows = jnp.where(mine & (lane % 4 == r), value, id_rows)
    ids_s[...] = id_rows.reshape(groups, 1, 128)
    target = jnp.where(active, owner * 8 + rank.astype(I32), -64)
    spot = lax.broadcasted_iota(I32, (groups * 8, n), 0)
    fresh_cp.wait()
    rows = jnp.zeros((groups * 8, HD), F32)
    for h in range(2):
        rows += dot(jnp.where(spot == target + 4 * h, 1.0, 0.0).astype(BF16), fresh[0, :, h * HD:(h + 1) * HD])
    send[...] = rows.astype(BF16).reshape(groups, 8, HD)

    pl.semaphore_wait(barrier, groups - 1 + ring - 1)

    piece = depth // 8
    order = [1, 7, 2, 6, 3, 5, 4]
    parts = ((0, 4), (4, 3))

    def piece_of(dx):
        return (lax.rem(x + dx + 4, 4) * 2 + core) * piece

    def wy_copy(p):
        to = y_peer(order[p])
        rows = pl.ds(pl.multiple_of(piece_of(0), piece), piece)
        return pltpu.make_async_remote_copy(
            w_hbm.at[rows, pl.ds(pl.multiple_of(to * cols, cols), cols)], wcol.at[p, rows],
            wy_s.at[p], wy_r.at[p], device_id={"tensor": to}, device_id_type=MESH)

    def wmove(kind, g):
        to_x = lambda dx: z * 8 + lax.rem(x + dx + 4, 4) * 2 + core
        dx, start, size, to = (
            (0, 0, piece, to_x(1)), (0, 0, piece, to_x(-1)),
            (-1, 0, piece // 2, to_x(1)), (1, piece // 2, piece // 2, to_x(-1)),
            (0, 0, piece, partner), (-1, 0, piece, partner), (1, 0, piece, partner), (2, 0, piece, partner),
        )[kind]
        at = wcol.at[pl.ds(*parts[g]), pl.ds(pl.multiple_of(piece_of(dx) + start, size), size)]
        return pltpu.make_async_remote_copy(
            at, at, wm_s.at[2 * kind + g], wm_r.at[2 * kind + g], device_id={"dp": to}, device_id_type=MESH)

    def pass_own(g):
        for p in range(parts[g][0], sum(parts[g])):
            wy_copy(p).wait_recv()
        for kind in (0, 1, 4):
            wmove(kind, g).start()

    def pass_sides(g):
        for side in (0, 1):
            wmove(side, g).wait_recv()
            wmove(2 + side, g).start()
            wmove(5 + side, g).start()

    def pass_last(g):
        wmove(2, g).wait_recv()
        wmove(3, g).wait_recv()
        wmove(7, g).start()

    def to_peer(src, dst, ss, rs, to):
        return pltpu.make_async_remote_copy(
            src.at[to], dst.at[me], ss, rs, device_id={"dp": to}, device_id_type=MESH)

    def whole(src, dst, ss, rs):
        return pltpu.make_async_remote_copy(
            src.at[pl.ds(0, groups - 1)], dst.at[pl.ds(0, groups - 1)], ss, rs,
            device_id={"dp": partner}, device_id_type=MESH)

    ids_x = (ids_s, ids_r, ids_ss, ids_rs)
    dat_x = (send, recv, dat_ss, dat_rs)
    lse_x = (lse_s, lse_r, lse_ss, lse_rs)
    ret_x = (rsend, rrecv, ret_ss, ret_rs)

    def go(to):
        to_peer(*ids_x, to).start()
        to_peer(*dat_x, to).start()

    for p in range(ring - 1):
        wy_copy(p).start()
    each_peer(go)
    keep = [pltpu.make_async_copy(a.at[me], b.at[me], lsem.at[7 + i]) for i, (a, b) in enumerate(
        ((ids_s, ids_r), (send, recv), (lse_s, lse_r), (rsend, rrecv)))]
    keep[0].start()
    keep[1].start()

    eye = lax.broadcasted_iota(I32, (n, n), 0) == lax.broadcasted_iota(I32, (n, n), 1)

    def as_column(row, wide):
        return dot(jnp.where(eye, row, 0).astype(BF16), jnp.ones((n, wide), BF16))

    lengths = as_column(len_ref[...].astype(F32), 16 * length)
    spot_col = (as_column(jnp.where(active, owner, -8).astype(F32), groups * 8) * 8
                + as_column(rank, groups * 8)).astype(I32)
    live[...] = jnp.where(spot_col[:, 0:HD] >= 0, 1.0, 0.0)
    spot_row = lax.broadcasted_iota(I32, (n, groups * 8), 1)
    scale = HD ** -0.5
    for h in range(2):
        cl = pl.ds(h * HD, HD)
        place[h] = jnp.where(spot_row == spot_col + 4 * h, 1.0, 0.0).astype(BF16)
        own = jnp.sum(fresh[0, :, cl].astype(F32) * fresh[1, :, cl].astype(F32), axis=1, keepdims=True) * scale
        own_sc[h] = jnp.broadcast_to(own, (n, HD))

    keep[0].wait()
    whole(*ids_x).wait_recv()

    def lanes_of(ref, b):
        total = ref[16 * b]
        for i in range(1, 16):
            total = total + ref[16 * b + i]
        return total

    slot = lax.broadcasted_iota(I32, (n, 128), 0) + 1
    half = (lax.broadcasted_iota(I32, (n, 128), 1) % 8) // 4
    for b in range(groups // 16):
        hit = lanes_of(ids_r, b).astype(I32) == slot
        for h in range(2):
            match[h, :, b * 128:(b + 1) * 128] = jnp.where(hit & (half == h), 1.0, 0.0).astype(BF16)
    keep[1].wait()
    whole(*dat_x).wait_recv()
    arrived = recv[...].reshape(groups * 8, HD)
    for h in range(2):
        owned[h] = dot(match[h], arrived).astype(BF16)

    kv_cp.wait()
    blocks = n // 16
    lane_i = lax.broadcasted_iota(I32, (n, 16 * length), 1)
    row_i = lax.broadcasted_iota(I32, (n, 16 * length), 0)
    valid = (lane_i // length == row_i % 16) & ((lane_i % length).astype(F32) < lengths)
    lse_row = jnp.zeros((1, groups * 8), F32)
    for h in range(2):
        cl = pl.ds(h * HD, HD)
        for i in range(blocks):
            keys = kv[16 * i:16 * i + 16, 0, :, cl].reshape(16 * length, HD)
            score[16 * i:16 * i + 16] = dot(owned[h, 16 * i:16 * i + 16], keys, 1, 1)
        s = jnp.where(valid, score[...] * scale, -1e30)
        top = jnp.max(s, axis=1, keepdims=True)
        e = jnp.where(valid, jnp.exp(s - top), 0.0)
        total = jnp.sum(e, axis=1, keepdims=True)
        w = (e / total).astype(BF16)
        lse_row += jnp.sum(match[h].astype(F32) * (top + jnp.log(total)), axis=0, keepdims=True)
        for i in range(blocks):
            values = kv[16 * i:16 * i + 16, 1, :, cl].reshape(16 * length, HD)
            att[h, 16 * i:16 * i + 16] = dot(w[16 * i:16 * i + 16], values).astype(BF16)
    back = dot(match[0], att[0], 0, 0) + dot(match[1], att[1], 0, 0)
    rsend[...] = back.astype(BF16).reshape(groups, 8, HD)
    spread = jnp.zeros((groups, 128), F32)
    group_i = lax.broadcasted_iota(I32, (groups, 128), 0)
    for b in range(groups // 16):
        spread = jnp.where(group_i // 16 == b, lse_row[:, b * 128:(b + 1) * 128], spread)
    lse_rows = jnp.zeros((groups, 128), F32)
    for i in range(8):
        value = jnp.sum(jnp.where(lane == (group_i % 16) * 8 + i, spread, 0.0), axis=1, keepdims=True)
        lse_rows = jnp.where(mine & (lane % 8 == i), value, lse_rows)
    lse_s[...] = lse_rows.reshape(groups, 1, 128)

    def go_back(to):
        to_peer(*lse_x, to).start()
        to_peer(*ret_x, to).start()

    each_peer(go_back)
    keep[2].start()
    keep[3].start()

    pass_own(0)
    pass_own(1)

    keep[2].wait()
    whole(*lse_x).wait_recv()
    lse_got = [lanes_of(lse_r, b) for b in range(groups // 16)]
    keep[3].wait()
    whole(*ret_x).wait_recv()
    back_rows = rrecv[...].reshape(groups * 8, HD)
    for h in range(2):
        cl = pl.ds(h * HD, HD)
        cached = dot(place[h], back_rows)
        lse = jnp.zeros((n, 128), F32)
        for b in range(groups // 16):
            lse += place[h, :, b * 128:(b + 1) * 128].astype(F32) * lse_got[b]
        lse = jnp.sum(lse, axis=1, keepdims=True)
        own = own_sc[h]
        top = jnp.maximum(lse, own)
        of_cache, of_own = jnp.exp(lse - top), jnp.exp(own - top)
        mixed = (of_cache * cached + of_own * fresh[2, :, cl].astype(F32)) / (of_cache + of_own)
        gath[y, :, cl] = (mixed * live[...]).astype(BF16)

    pieces = 4
    hr = n // pieces

    def ring_copy(s, q, way):
        src = lax.rem(y + (ring - s if way > 0 else s), ring)
        to = lax.rem(y + (1 if way > 0 else ring - 1), ring)
        at = gath.at[src, pl.ds(q * hr, hr)]
        i = (s * pieces + q) * 2 + (way > 0)
        return pltpu.make_async_remote_copy(
            at, at, ag_s.at[i], ag_r.at[i], device_id={"tensor": to}, device_id_type=MESH)

    last = ring // 2 - 1
    moves = [(s, q if way > 0 else pieces - 1 - q, way)
             for s in range(last + 1) for q in range(pieces) for way in (1, -1)
             if s < last or q < pieces // 2]
    for m in moves:
        if m[0] == 0:
            ring_copy(*m).start()

    pass_sides(0)
    pass_sides(1)

    def relay(s):
        for m in moves:
            if m[0] == s:
                ring_copy(*m).wait_recv()
                nxt = (s + 1, m[1], m[2])
                if nxt in moves:
                    ring_copy(*nxt).start()

    def project(d):
        return dot(gath[lax.rem(y + ring - d, ring)], wcol[order.index(d)])

    relay(0)
    pass_last(0)
    pass_last(1)
    wown_cp.wait()
    res_cp.wait()
    acc[...] = res[...].astype(F32) + dot(gath[y], wcol[ring - 1])
    relay(1)
    for g in range(2):
        for kind in range(4, 8):
            wmove(kind, g).wait_recv()
    acc[...] += project(1) + project(ring - 1)
    relay(2)
    acc[...] += project(2) + project(ring - 2)
    acc[...] += project(3) + project(ring - 3)
    relay(3)
    out_ref[...] = (acc[...] + project(4)).astype(BF16)

    for ex in (ids_x, dat_x, lse_x, ret_x):
        whole(*ex).wait_send()
    for p in range(ring - 1):
        wy_copy(p).wait_send()
    for g in range(2):
        for kind in range(8):
            wmove(kind, g).wait_send()
    for m in moves:
        ring_copy(*m).wait_send()


def body(groups, ring, residual, fresh_qkv, active, home_slot, kv_cache, lengths, w_out):
    n = home_slot.shape[0]
    width = fresh_qkv.shape[2]
    cols = residual.shape[1]
    depth = w_out.shape[0]
    length = kv_cache.shape[2]
    hbm = pl.BlockSpec(memory_space=pl.ANY)
    dma = pltpu.SemaphoreType.DMA
    return pl.pallas_call(
        functools.partial(kernel, groups, ring),
        out_shape=jax.ShapeDtypeStruct((n, cols), BF16),
        in_specs=[hbm] * 7,
        out_specs=pl.BlockSpec(memory_space=pltpu.VMEM),
        scratch_shapes=[
            pltpu.VMEM((3, n, width), BF16),
            pltpu.VMEM((1, n), I32),
            pltpu.VMEM((1, n), I32),
            pltpu.VMEM((1, n), I32),
            pltpu.VMEM(kv_cache.shape, BF16),
            pltpu.VMEM((ring, depth, cols), BF16),
            pltpu.VMEM((n, cols), BF16),
            pltpu.VMEM((groups, 1, 128), F32),
            pltpu.VMEM((groups, 1, 128), F32),
            pltpu.VMEM((groups, 8, HD), BF16),
            pltpu.VMEM((groups, 8, HD), BF16),
            pltpu.VMEM((groups, 8, HD), BF16),
            pltpu.VMEM((groups, 8, HD), BF16),
            pltpu.VMEM((groups, 1, 128), F32),
            pltpu.VMEM((groups, 1, 128), F32),
            pltpu.VMEM((ring, n, width), BF16),
            pltpu.VMEM((2, n, groups * 8), BF16),
            pltpu.VMEM((2, n, groups * 8), BF16),
            pltpu.VMEM((2, n, HD), BF16),
            pltpu.VMEM((n, 16 * length), F32),
            pltpu.VMEM((2, n, HD), BF16),
            pltpu.VMEM((2, n, HD), F32),
            pltpu.VMEM((n, HD), F32),
            pltpu.VMEM((n, cols), F32),
            dma((11,)),
            dma, dma, dma, dma, dma, dma, dma, dma,
            dma((ring,)), dma((ring,)), dma((16,)), dma((16,)), dma((32,)), dma((32,)),
        ],
        compiler_params=pltpu.CompilerParams(collective_id=0, has_side_effects=True),
    )(
        fresh_qkv.transpose(1, 0, 2), active.reshape(1, n), home_slot.reshape(1, n), lengths.reshape(1, n),
        kv_cache, w_out, residual,
    )


def solution(mesh):
    placed = (
        P("dp", "tensor"),
        P("dp", None, "tensor"),
        P("dp"),
        P("dp"),
        P("dp", None, None, "tensor"),
        P("dp"),
        P("tensor", None),
    )
    return jax.shard_map(
        functools.partial(body, mesh.shape["dp"], mesh.shape["tensor"]),
        mesh=mesh, in_specs=placed, out_specs=P("dp", "tensor"), check_vma=False,
    )
```

time: 58.7 us -> 49.7 us (0.85)
  the two profiles are of different devices: /device:TPU:4 before, /device:TPU:16 now
where the time goes in v2:
time: 49.7 us; the launch traced here: 49.5 us
  Pallas kernels  47.9 us (96%)
  local copies, waits for them, and re-layouts  1.67 us (3%)
    pallas_call x1, Pallas kernels, body(): pl.pallas_call(functools.partial(kernel, groups, ring), out_shape=jax.Sha...  47.9 us
    unnamed x1, local copies, waits for them, and re-layouts  1.67 us

profile of v2, /device:TPU:16, one launch (start us, length us, event | category | flops | bytes accessed | tf_op | source)
XLA Modules:
  0.0 49.5 jit_solution(5319047971400945566)
XLA Ops:
  0.0 47.9 %shard_map.73 = bf16[256,512]{1,0:T(8,128)(2,1)} custom-call(bf16[3,256,256]{2,1,0:T(8,128)(2,1)} %bitcast.4, s32[1,256]{1,0:T(1,128)} %bitcast.5, s32[1,256]{1,0:T(1,128)} %bitcast.6, s32[1,256]{1,0:T(1,128)} %bitcast.7, bf16[256,2,16,256]{3,2,1,0:T(8,128)(2,1)} %kv_hbm.1, bf16[256,4096]{1,0:T(8,128)(2,1)} %w_hbm.1, bf16[256,512]{1,0:T(8,128)(2,1)} %res_hbm.1), custom_call_target="tpu_custom_call" | custom-call | tf_op jit(solution)/shard_map/pallas_call | solution.py:344
  47.9 1.7 %copy.9 = bf16[256,512]{1,0:T(8,128)(2,1)} copy(bf16[256,512]{1,0:T(8,128)(2,1)} %shard_map.73) | data formatting | bytes 524288

commit v3 on v2

--- a/solution.py
+++ b/solution.py
@@ -21,11 +21,11 @@
     groups, ring,
     fresh_hbm, act_hbm, home_hbm, len_hbm, kv_hbm, w_hbm, res_hbm,
     out_ref,
-    fresh, act_ref, home_ref, len_ref, kv, wcol, res, ids_s, ids_r, send, recv, rsend, rrecv, lse_s, lse_r,
+    fresh, small, kv, wcol, res, ids_s, ids_r, send, recv, rsend, rrecv, lse_s, lse_r,
     gath, place, match, owned, score, att, own_sc, live, acc,
-    lsem, ids_ss, ids_rs, dat_ss, dat_rs, lse_ss, lse_rs, ret_ss, ret_rs, wy_s, wy_r, wm_s, wm_r, ag_s, ag_r,
+    lsem, ids_ss, ids_rs, dat_ss, dat_rs, lse_ss, lse_rs, ret_ss, ret_rs, w_sem, wy_r, wm_r, ag_s, ag_r,
 ):
-    n = act_ref.shape[1]
+    n = small.shape[2]
     length = kv.shape[2]
     cols = wcol.shape[2]
     depth = wcol.shape[1]
@@ -57,27 +57,24 @@
     def greet(to):
         pl.semaphore_signal(barrier, inc=1, device_id={"dp": to}, device_id_type=MESH)
 
-    small = [pltpu.make_async_copy(a, b, lsem.at[i]) for i, (a, b) in enumerate(
-        ((home_hbm, home_ref), (act_hbm, act_ref), (len_hbm, len_ref)))]
-    for cp in small:
-        cp.start()
-    fresh_cp = pltpu.make_async_copy(fresh_hbm, fresh, lsem.at[3])
+    for i, a in enumerate((home_hbm, act_hbm, len_hbm)):
+        pltpu.make_async_copy(a, small.at[i], lsem.at[0]).start()
+    fresh_cp = pltpu.make_async_copy(fresh_hbm, fresh, lsem.at[1])
     fresh_cp.start()
     each_peer(greet)
     for d in range(1, ring):
         pl.semaphore_signal(barrier, inc=1, device_id={"tensor": y_peer(d)}, device_id_type=MESH)
-    kv_cp = pltpu.make_async_copy(kv_hbm, kv, lsem.at[4])
+    kv_cp = pltpu.make_async_copy(kv_hbm, kv, lsem.at[2])
     kv_cp.start()
     wown_cp = pltpu.make_async_copy(
-        w_hbm.at[:, pl.ds(pl.multiple_of(y * cols, cols), cols)], wcol.at[ring - 1], lsem.at[5])
+        w_hbm.at[:, pl.ds(pl.multiple_of(y * cols, cols), cols)], wcol.at[ring - 1], lsem.at[3])
     wown_cp.start()
-    res_cp = pltpu.make_async_copy(res_hbm, res, lsem.at[6])
+    res_cp = pltpu.make_async_copy(res_hbm, res, lsem.at[4])
     res_cp.start()
 
-    for cp in small:
-        cp.wait()
-    home = home_ref[...]
-    active = act_ref[...] > 0
+    pltpu.make_async_copy(small, small, lsem.at[0]).wait()
+    home = small[0]
+    active = small[1] > 0
     owner = home // n
     local_id = (home - owner * n + 1).astype(F32)
     of_group = (owner == lax.broadcasted_iota(I32, (groups, n), 0)) & active
@@ -116,9 +113,10 @@
         rows = pl.ds(pl.multiple_of(piece_of(0), piece), piece)
         return pltpu.make_async_remote_copy(
             w_hbm.at[rows, pl.ds(pl.multiple_of(to * cols, cols), cols)], wcol.at[p, rows],
-            wy_s.at[p], wy_r.at[p], device_id={"tensor": to}, device_id_type=MESH)
+            w_sem, wy_r.at[int(p >= parts[1][0])], device_id={"tensor": to}, device_id_type=MESH)
 
     def wmove(kind, g):
+        slot_of = (0, 2, 4, 4, 6, 6, 6, 6)
         to_x = lambda dx: z * 8 + lax.rem(x + dx + 4, 4) * 2 + core
         dx, start, size, to = (
             (0, 0, piece, to_x(1)), (0, 0, piece, to_x(-1)),
@@ -127,11 +125,15 @@
         )[kind]
         at = wcol.at[pl.ds(*parts[g]), pl.ds(pl.multiple_of(piece_of(dx) + start, size), size)]
         return pltpu.make_async_remote_copy(
-            at, at, wm_s.at[2 * kind + g], wm_r.at[2 * kind + g], device_id={"dp": to}, device_id_type=MESH)
+            at, at, w_sem, wm_r.at[slot_of[kind] + (g if kind < 4 else 0)], device_id={"dp": to}, device_id_type=MESH)
+
+    def w_all(recv_sem, rows, first, count):
+        at = wcol.at[pl.ds(first, count), pl.ds(0, rows)]
+        return pltpu.make_async_remote_copy(
+            at, at, w_sem, recv_sem, device_id={"dp": partner}, device_id_type=MESH)
 
     def pass_own(g):
-        for p in range(parts[g][0], sum(parts[g])):
-            wy_copy(p).wait_recv()
+        w_all(wy_r.at[g], piece, *parts[g]).wait_recv()
         for kind in (0, 1, 4):
             wmove(kind, g).start()
 
@@ -142,8 +144,7 @@
             wmove(5 + side, g).start()
 
     def pass_last(g):
-        wmove(2, g).wait_recv()
-        wmove(3, g).wait_recv()
+        w_all(wm_r.at[4 + g], piece, *parts[g]).wait_recv()
         wmove(7, g).start()
 
     def to_peer(src, dst, ss, rs, to):
@@ -167,7 +168,7 @@
     for p in range(ring - 1):
         wy_copy(p).start()
     each_peer(go)
-    keep = [pltpu.make_async_copy(a.at[me], b.at[me], lsem.at[7 + i]) for i, (a, b) in enumerate(
+    keep = [pltpu.make_async_copy(a.at[me], b.at[me], lsem.at[5 + i]) for i, (a, b) in enumerate(
         ((ids_s, ids_r), (send, recv), (lse_s, lse_r), (rsend, rrecv)))]
     keep[0].start()
     keep[1].start()
@@ -177,7 +178,7 @@
     def as_column(row, wide):
         return dot(jnp.where(eye, row, 0).astype(BF16), jnp.ones((n, wide), BF16))
 
-    lengths = as_column(len_ref[...].astype(F32), 16 * length)
+    lengths = as_column(small[2].astype(F32), 16 * length)
     spot_col = (as_column(jnp.where(active, owner, -8).astype(F32), groups * 8) * 8
                 + as_column(rank, groups * 8)).astype(I32)
     live[...] = jnp.where(spot_col[:, 0:HD] >= 0, 1.0, 0.0)
@@ -281,7 +282,7 @@
         at = gath.at[src, pl.ds(q * hr, hr)]
         i = (s * pieces + q) * 2 + (way > 0)
         return pltpu.make_async_remote_copy(
-            at, at, ag_s.at[i], ag_r.at[i], device_id={"tensor": to}, device_id_type=MESH)
+            at, at, ag_s, ag_r.at[i], device_id={"tensor": to}, device_id_type=MESH)
 
     last = ring // 2 - 1
     moves = [(s, q if way > 0 else pieces - 1 - q, way)
@@ -312,9 +313,7 @@
     res_cp.wait()
     acc[...] = res[...].astype(F32) + dot(gath[y], wcol[ring - 1])
     relay(1)
-    for g in range(2):
-        for kind in range(4, 8):
-            wmove(kind, g).wait_recv()
+    w_all(wm_r.at[6], depth // 2, 0, ring - 1).wait_recv()
     acc[...] += project(1) + project(ring - 1)
     relay(2)
     acc[...] += project(2) + project(ring - 2)
@@ -324,13 +323,10 @@
 
     for ex in (ids_x, dat_x, lse_x, ret_x):
         whole(*ex).wait_send()
-    for p in range(ring - 1):
-        wy_copy(p).wait_send()
-    for g in range(2):
-        for kind in range(8):
-            wmove(kind, g).wait_send()
-    for m in moves:
-        ring_copy(*m).wait_send()
+    w_all(wm_r.at[6], depth, 0, ring - 1).wait_send()
+    ring_all = gath.at[pl.ds(0, ring - 1)]
+    pltpu.make_async_remote_copy(
+        ring_all, ring_all, ag_s, ag_r.at[0], device_id={"tensor": y_peer(1)}, device_id_type=MESH).wait_send()
 
 
 def body(groups, ring, residual, fresh_qkv, active, home_slot, kv_cache, lengths, w_out):
@@ -348,9 +344,7 @@
         out_specs=pl.BlockSpec(memory_space=pltpu.VMEM),
         scratch_shapes=[
             pltpu.VMEM((3, n, width), BF16),
-            pltpu.VMEM((1, n), I32),
-            pltpu.VMEM((1, n), I32),
-            pltpu.VMEM((1, n), I32),
+            pltpu.VMEM((3, 1, n), I32),
             pltpu.VMEM(kv_cache.shape, BF16),
             pltpu.VMEM((ring, depth, cols), BF16),
             pltpu.VMEM((n, cols), BF16),
@@ -371,9 +365,9 @@
             pltpu.VMEM((2, n, HD), F32),
             pltpu.VMEM((n, HD), F32),
             pltpu.VMEM((n, cols), F32),
-            dma((11,)),
+            dma((9,)),
             dma, dma, dma, dma, dma, dma, dma, dma,
-            dma((ring,)), dma((ring,)), dma((16,)), dma((16,)), dma((32,)), dma((32,)),
+            dma, dma((2,)), dma((7,)), dma, dma((32,)),
         ],
         compiler_params=pltpu.CompilerParams(collective_id=0, has_side_effects=True),
     )(

time: 49.7 us -> 49 us (0.986)
  Pallas kernels: 47.9 us -> 47.1 us
    pallas_call x1, Pallas kernels: 47.9 us -> 47.1 us  [body(): pl.pallas_call(functools.partial(kernel, groups, ring), out_shape=jax.Sha...]
where the time goes in v3:
time: 49 us; the launch traced here: 48.8 us
  Pallas kernels  47.1 us (96%)
  local copies, waits for them, and re-layouts  1.67 us (3%)
    pallas_call x1, Pallas kernels, body(): pl.pallas_call(functools.partial(kernel, groups, ring), out_shape=jax.Sha...  47.1 us
    unnamed x1, local copies, waits for them, and re-layouts  1.67 us

profile of v3, /device:TPU:16, one launch (start us, length us, event | category | flops | bytes accessed | tf_op | source)
XLA Modules:
  0.0 48.8 jit_solution(17379468921315860798)
XLA Ops:
  0.0 47.1 %shard_map.73 = bf16[256,512]{1,0:T(8,128)(2,1)} custom-call(bf16[3,256,256]{2,1,0:T(8,128)(2,1)} %bitcast.4, s32[1,256]{1,0:T(1,128)} %bitcast.5, s32[1,256]{1,0:T(1,128)} %bitcast.6, s32[1,256]{1,0:T(1,128)} %bitcast.7, bf16[256,2,16,256]{3,2,1,0:T(8,128)(2,1)} %kv_hbm.1, bf16[256,4096]{1,0:T(8,128)(2,1)} %w_hbm.1, bf16[256,512]{1,0:T(8,128)(2,1)} %res_hbm.1), custom_call_target="tpu_custom_call" | custom-call | tf_op jit(solution)/shard_map/pallas_call | solution.py:340
  47.2 1.7 %copy.9 = bf16[256,512]{1,0:T(8,128)(2,1)} copy(bf16[256,512]{1,0:T(8,128)(2,1)} %shard_map.73) | data formatting | bytes 524288

commit v4 on v3

--- a/solution.py
+++ b/solution.py
@@ -21,9 +21,9 @@
     groups, ring,
     fresh_hbm, act_hbm, home_hbm, len_hbm, kv_hbm, w_hbm, res_hbm,
     out_ref,
-    fresh, small, kv, wcol, res, ids_s, ids_r, send, recv, rsend, rrecv, lse_s, lse_r,
-    gath, place, match, owned, score, att, own_sc, live, acc,
-    lsem, ids_ss, ids_rs, dat_ss, dat_rs, lse_ss, lse_rs, ret_ss, ret_rs, w_sem, wy_r, wm_r, ag_s, ag_r,
+    fresh, small, kv, wcol, res, send, recv, rsend, rrecv,
+    gath, place, match, owned, score, att, own_sc, live, of_owner, of_row, acc, done,
+    lsem, dat_ss, dat_rs, ret_ss, ret_rs, w_sem, wy_r, wm_r, ag_s, ag_r,
 ):
     n = small.shape[2]
     length = kv.shape[2]
@@ -35,19 +35,18 @@
     z, x, core = me // 8, lax.rem(me, 8) // 2, lax.rem(me, 2)
     partner = me + 1 - 2 * core
 
-    beside = [lax.rem(me + m, 8) for m in range(8)]
+    plane_at = [lax.rem(z + dz, planes) * 8 for dz in range(planes)]
+    chip_at = [lax.rem(x + dx, 4) * 2 for dx in range(4)]
+    hops = lambda dz, dx: min(dz, planes - dz) + min(dx, 4 - dx)
+    far_first = sorted(
+        ((dz, dx) for dz in range(planes) for dx in range(4)),
+        key=lambda p: (-hops(*p), abs(p[0] - planes // 2)))
 
     def each_peer(act):
-        def plane(i, c):
-            dz = planes // 2 + (1 - 2 * lax.rem(i, 2)) * ((i + 1) // 2)
-            base = lax.rem(z + dz, planes) * 8
-            for m in range(8):
-                act(base + beside[7 - m])
-            return c
-
-        lax.fori_loop(0, planes - 1, plane, 0)
-        for m in range(7):
-            act(z * 8 + beside[7 - m])
+        for dz, dx in far_first[:-1]:
+            for c in range(2):
+                act(plane_at[dz] + chip_at[dx] + c)
+        act(partner)
 
     def y_peer(d):
         return lax.rem(y + d, ring)
@@ -90,14 +89,19 @@
     for r in range(CAP):
         value = jnp.sum(jnp.where(rank == r, one_hot * local_id, 0.0), axis=1, keepdims=True)
         id_rows = jnp.where(mine & (lane % 4 == r), value, id_rows)
-    ids_s[...] = id_rows.reshape(groups, 1, 128)
+    first_row = lax.broadcasted_iota(I32, (groups, 2, 128), 1) == 0
+
+    def fifth(rows):
+        return jnp.where(first_row, jnp.broadcast_to(rows.reshape(groups, 1, 128), (groups, 2, 128)), 0.0).astype(BF16)
+
+    send[:, 4] = fifth(id_rows)
     target = jnp.where(active, owner * 8 + rank.astype(I32), -64)
     spot = lax.broadcasted_iota(I32, (groups * 8, n), 0)
     fresh_cp.wait()
     rows = jnp.zeros((groups * 8, HD), F32)
     for h in range(2):
         rows += dot(jnp.where(spot == target + 4 * h, 1.0, 0.0).astype(BF16), fresh[0, :, h * HD:(h + 1) * HD])
-    send[...] = rows.astype(BF16).reshape(groups, 8, HD)
+    send[:, 0:4] = rows.astype(BF16).reshape(groups, 4, 2, HD)
 
     pl.semaphore_wait(barrier, groups - 1 + ring - 1)
 
@@ -156,22 +160,15 @@
             src.at[pl.ds(0, groups - 1)], dst.at[pl.ds(0, groups - 1)], ss, rs,
             device_id={"dp": partner}, device_id_type=MESH)
 
-    ids_x = (ids_s, ids_r, ids_ss, ids_rs)
     dat_x = (send, recv, dat_ss, dat_rs)
-    lse_x = (lse_s, lse_r, lse_ss, lse_rs)
     ret_x = (rsend, rrecv, ret_ss, ret_rs)
-
-    def go(to):
-        to_peer(*ids_x, to).start()
-        to_peer(*dat_x, to).start()
 
     for p in range(ring - 1):
         wy_copy(p).start()
-    each_peer(go)
+    each_peer(lambda to: to_peer(*dat_x, to).start())
     keep = [pltpu.make_async_copy(a.at[me], b.at[me], lsem.at[5 + i]) for i, (a, b) in enumerate(
-        ((ids_s, ids_r), (send, recv), (lse_s, lse_r), (rsend, rrecv)))]
+        ((send, recv), (rsend, rrecv)))]
     keep[0].start()
-    keep[1].start()
 
     eye = lax.broadcasted_iota(I32, (n, n), 0) == lax.broadcasted_iota(I32, (n, n), 1)
 
@@ -179,35 +176,32 @@
         return dot(jnp.where(eye, row, 0).astype(BF16), jnp.ones((n, wide), BF16))
 
     lengths = as_column(small[2].astype(F32), 16 * length)
-    spot_col = (as_column(jnp.where(active, owner, -8).astype(F32), groups * 8) * 8
-                + as_column(rank, groups * 8)).astype(I32)
+    owner_col = as_column(jnp.where(active, owner, -8).astype(F32), groups * 8)
+    rank_col = as_column(rank, groups * 8)
+    spot_col = (owner_col * 8 + rank_col).astype(I32)
+    lane_n = lax.broadcasted_iota(I32, (n, HD), 1)
+    of_owner[...] = jnp.where(lane_n == owner_col[:, 0:HD].astype(I32) * 2, 1.0, 0.0).astype(BF16)
     live[...] = jnp.where(spot_col[:, 0:HD] >= 0, 1.0, 0.0)
     spot_row = lax.broadcasted_iota(I32, (n, groups * 8), 1)
     scale = HD ** -0.5
     for h in range(2):
         cl = pl.ds(h * HD, HD)
+        of_row[h] = jnp.where(
+            (lane_n % 8 == rank_col[:, 0:HD].astype(I32) + 4 * h) & (lane_n < 24), 1.0, 0.0).astype(F32)
         place[h] = jnp.where(spot_row == spot_col + 4 * h, 1.0, 0.0).astype(BF16)
         own = jnp.sum(fresh[0, :, cl].astype(F32) * fresh[1, :, cl].astype(F32), axis=1, keepdims=True) * scale
         own_sc[h] = jnp.broadcast_to(own, (n, HD))
 
     keep[0].wait()
-    whole(*ids_x).wait_recv()
-
-    def lanes_of(ref, b):
-        total = ref[16 * b]
-        for i in range(1, 16):
-            total = total + ref[16 * b + i]
-        return total
-
+    whole(*dat_x).wait_recv()
+    got_ids = recv[:, 4].reshape(groups * 2, 128).astype(F32)
     slot = lax.broadcasted_iota(I32, (n, 128), 0) + 1
     half = (lax.broadcasted_iota(I32, (n, 128), 1) % 8) // 4
     for b in range(groups // 16):
-        hit = lanes_of(ids_r, b).astype(I32) == slot
+        hit = jnp.sum(got_ids[32 * b:32 * b + 32], axis=0, keepdims=True).astype(I32) == slot
         for h in range(2):
             match[h, :, b * 128:(b + 1) * 128] = jnp.where(hit & (half == h), 1.0, 0.0).astype(BF16)
-    keep[1].wait()
-    whole(*dat_x).wait_recv()
-    arrived = recv[...].reshape(groups * 8, HD)
+    arrived = recv[:, 0:4].reshape(groups * 8, HD)
     for h in range(2):
         owned[h] = dot(match[h], arrived).astype(BF16)
 
@@ -216,23 +210,31 @@
     lane_i = lax.broadcasted_iota(I32, (n, 16 * length), 1)
     row_i = lax.broadcasted_iota(I32, (n, 16 * length), 0)
     valid = (lane_i // length == row_i % 16) & ((lane_i % length).astype(F32) < lengths)
-    lse_row = jnp.zeros((1, groups * 8), F32)
+    none = jnp.zeros((16, HD), BF16)
+    for i in range(blocks):
+        rows = slice(16 * i, 16 * i + 16)
+        query = jnp.concatenate([
+            jnp.concatenate([owned[0, rows], none], axis=1), jnp.concatenate([none, owned[1, rows]], axis=1)], axis=0)
+        both = dot(query, kv[rows, 0].reshape(16 * length, 2 * HD), 1, 1)
+        score[0, rows] = both[0:16]
+        score[1, rows] = both[16:32]
+    lse_of, weights = [], []
     for h in range(2):
-        cl = pl.ds(h * HD, HD)
-        for i in range(blocks):
-            keys = kv[16 * i:16 * i + 16, 0, :, cl].reshape(16 * length, HD)
-            score[16 * i:16 * i + 16] = dot(owned[h, 16 * i:16 * i + 16], keys, 1, 1)
-        s = jnp.where(valid, score[...] * scale, -1e30)
+        s = jnp.where(valid, score[h] * scale, -1e30)
         top = jnp.max(s, axis=1, keepdims=True)
         e = jnp.where(valid, jnp.exp(s - top), 0.0)
         total = jnp.sum(e, axis=1, keepdims=True)
-        w = (e / total).astype(BF16)
-        lse_row += jnp.sum(match[h].astype(F32) * (top + jnp.log(total)), axis=0, keepdims=True)
-        for i in range(blocks):
-            values = kv[16 * i:16 * i + 16, 1, :, cl].reshape(16 * length, HD)
-            att[h, 16 * i:16 * i + 16] = dot(w[16 * i:16 * i + 16], values).astype(BF16)
+        weights.append((e * (1.0 / total)).astype(BF16))
+        lse_of.append(top + jnp.log(total))
+    for i in range(blocks):
+        rows = slice(16 * i, 16 * i + 16)
+        both = dot(jnp.concatenate([weights[0][rows], weights[1][rows]], axis=0), kv[rows, 1].reshape(16 * length, 2 * HD))
+        att[0, rows] = both[0:16, 0:HD].astype(BF16)
+        att[1, rows] = both[16:32, HD:2 * HD].astype(BF16)
+    lse_row = jnp.sum(
+        match[0].astype(F32) * lse_of[0] + match[1].astype(F32) * lse_of[1], axis=0, keepdims=True)
     back = dot(match[0], att[0], 0, 0) + dot(match[1], att[1], 0, 0)
-    rsend[...] = back.astype(BF16).reshape(groups, 8, HD)
+    rsend[:, 0:4] = back.astype(BF16).reshape(groups, 4, 2, HD)
     spread = jnp.zeros((groups, 128), F32)
     group_i = lax.broadcasted_iota(I32, (groups, 128), 0)
     for b in range(groups // 16):
@@ -240,39 +242,21 @@
     lse_rows = jnp.zeros((groups, 128), F32)
     for i in range(8):
         value = jnp.sum(jnp.where(lane == (group_i % 16) * 8 + i, spread, 0.0), axis=1, keepdims=True)
-        lse_rows = jnp.where(mine & (lane % 8 == i), value, lse_rows)
-    lse_s[...] = lse_rows.reshape(groups, 1, 128)
-
-    def go_back(to):
-        to_peer(*lse_x, to).start()
-        to_peer(*ret_x, to).start()
-
-    each_peer(go_back)
-    keep[2].start()
-    keep[3].start()
+        lse_rows = jnp.where(lane % 8 == i, value, lse_rows)
+    high = lse_rows.astype(BF16).astype(F32)
+    middle = (lse_rows - high).astype(BF16).astype(F32)
+    low = lse_rows - high - middle
+    terms = jnp.where(lane < 8, high, jnp.where(lane < 16, middle, jnp.where(lane < 24, low, 0.0)))
+    rsend[:, 4] = fifth(terms)
+
+    each_peer(lambda to: to_peer(*ret_x, to).start())
+    keep[1].start()
 
     pass_own(0)
     pass_own(1)
 
-    keep[2].wait()
-    whole(*lse_x).wait_recv()
-    lse_got = [lanes_of(lse_r, b) for b in range(groups // 16)]
-    keep[3].wait()
+    keep[1].wait()
     whole(*ret_x).wait_recv()
-    back_rows = rrecv[...].reshape(groups * 8, HD)
-    for h in range(2):
-        cl = pl.ds(h * HD, HD)
-        cached = dot(place[h], back_rows)
-        lse = jnp.zeros((n, 128), F32)
-        for b in range(groups // 16):
-            lse += place[h, :, b * 128:(b + 1) * 128].astype(F32) * lse_got[b]
-        lse = jnp.sum(lse, axis=1, keepdims=True)
-        own = own_sc[h]
-        top = jnp.maximum(lse, own)
-        of_cache, of_own = jnp.exp(lse - top), jnp.exp(own - top)
-        mixed = (of_cache * cached + of_own * fresh[2, :, cl].astype(F32)) / (of_cache + of_own)
-        gath[y, :, cl] = (mixed * live[...]).astype(BF16)
-
     pieces = 4
     hr = n // pieces
 
@@ -288,9 +272,33 @@
     moves = [(s, q if way > 0 else pieces - 1 - q, way)
              for s in range(last + 1) for q in range(pieces) for way in (1, -1)
              if s < last or q < pieces // 2]
-    for m in moves:
-        if m[0] == 0:
-            ring_copy(*m).start()
+    back_rows = rrecv[:, 0:4].reshape(groups * 8, HD)
+    term_rows = rrecv[:, 4].reshape(groups * 2, 128)
+
+    def settle(q):
+        rows = pl.ds(q * hr, hr)
+        lse_terms = dot(of_owner[rows], term_rows)
+        for h in range(2):
+            cl = pl.ds(h * HD, HD)
+            cached = dot(place[h, rows], back_rows)
+            lse = jnp.sum(lse_terms * of_row[h, rows], axis=1, keepdims=True)
+            own = own_sc[h, rows]
+            top = jnp.maximum(lse, own)
+            of_cache, of_own = jnp.exp(lse - top), jnp.exp(own - top)
+            mixed = (of_cache * cached + of_own * fresh[2, rows, cl].astype(F32)) / (of_cache + of_own)
+            gath[y, rows, cl] = (mixed * live[rows]).astype(BF16)
+
+    settle(0)
+    ring_copy(0, 0, 1).start()
+    settle(3)
+    ring_copy(0, 3, -1).start()
+    settle(1)
+    ring_copy(0, 1, 1).start()
+    settle(2)
+    ring_copy(0, 2, -1).start()
+    for q in (2, 3):
+        ring_copy(0, q, 1).start()
+        ring_copy(0, 3 - q, -1).start()
 
     pass_sides(0)
     pass_sides(1)
@@ -318,15 +326,21 @@
     relay(2)
     acc[...] += project(2) + project(ring - 2)
     acc[...] += project(3) + project(ring - 3)
-    relay(3)
-    out_ref[...] = (acc[...] + project(4)).astype(BF16)
-
-    for ex in (ids_x, dat_x, lse_x, ret_x):
+    farthest = lax.rem(y + ring // 2, ring)
+    for m in moves:
+        if m[0] == last:
+            ring_copy(*m).wait_recv()
+            rows = pl.ds(m[1] * hr, hr)
+            done[rows] = (acc[rows] + dot(gath[farthest, rows], wcol[order.index(ring // 2)])).astype(BF16)
+            pltpu.make_async_copy(done.at[rows], out_ref.at[rows], lsem.at[7]).start()
+
+    for ex in (dat_x, ret_x):
         whole(*ex).wait_send()
     w_all(wm_r.at[6], depth, 0, ring - 1).wait_send()
     ring_all = gath.at[pl.ds(0, ring - 1)]
     pltpu.make_async_remote_copy(
         ring_all, ring_all, ag_s, ag_r.at[0], device_id={"tensor": y_peer(1)}, device_id_type=MESH).wait_send()
+    pltpu.make_async_copy(done, out_ref, lsem.at[7]).wait()
 
 
 def body(groups, ring, residual, fresh_qkv, active, home_slot, kv_cache, lengths, w_out):
@@ -341,32 +355,31 @@
         functools.partial(kernel, groups, ring),
         out_shape=jax.ShapeDtypeStruct((n, cols), BF16),
         in_specs=[hbm] * 7,
-        out_specs=pl.BlockSpec(memory_space=pltpu.VMEM),
+        out_specs=hbm,
         scratch_shapes=[
             pltpu.VMEM((3, n, width), BF16),
             pltpu.VMEM((3, 1, n), I32),
             pltpu.VMEM(kv_cache.shape, BF16),
             pltpu.VMEM((ring, depth, cols), BF16),
             pltpu.VMEM((n, cols), BF16),
-            pltpu.VMEM((groups, 1, 128), F32),
-            pltpu.VMEM((groups, 1, 128), F32),
-            pltpu.VMEM((groups, 8, HD), BF16),
-            pltpu.VMEM((groups, 8, HD), BF16),
-            pltpu.VMEM((groups, 8, HD), BF16),
-            pltpu.VMEM((groups, 8, HD), BF16),
-            pltpu.VMEM((groups, 1, 128), F32),
-            pltpu.VMEM((groups, 1, 128), F32),
+            pltpu.VMEM((groups, 5, 2, HD), BF16),
+            pltpu.VMEM((groups, 5, 2, HD), BF16),
+            pltpu.VMEM((groups, 5, 2, HD), BF16),
+            pltpu.VMEM((groups, 5, 2, HD), BF16),
             pltpu.VMEM((ring, n, width), BF16),
             pltpu.VMEM((2, n, groups * 8), BF16),
             pltpu.VMEM((2, n, groups * 8), BF16),
             pltpu.VMEM((2, n, HD), BF16),
-            pltpu.VMEM((n, 16 * length), F32),
+            pltpu.VMEM((2, n, 16 * length), F32),
             pltpu.VMEM((2, n, HD), BF16),
             pltpu.VMEM((2, n, HD), F32),
             pltpu.VMEM((n, HD), F32),
+            pltpu.VMEM((n, HD), BF16),
+            pltpu.VMEM((2, n, HD), F32),
             pltpu.VMEM((n, cols), F32),
-            dma((9,)),
-            dma, dma, dma, dma, dma, dma, dma, dma,
+            pltpu.VMEM((n, cols), BF16),
+            dma((8,)),
+            dma, dma, dma, dma,
             dma, dma((2,)), dma((7,)), dma, dma((32,)),
         ],
         compiler_params=pltpu.CompilerParams(collective_id=0, has_side_effects=True),

time: 49 us -> 48.7 us (level)
  no operation moved by 1% of the time
where the time goes in v4:
time: 48.7 us; the launch traced here: 48.5 us
  Pallas kernels  46.8 us (96%)
  local copies, waits for them, and re-layouts  1.67 us (3%)
    pallas_call x1, Pallas kernels, body(): pl.pallas_call(functools.partial(kernel, groups, ring), out_shape=jax.Sha...  46.8 us
    unnamed x1, local copies, waits for them, and re-layouts  1.67 us

profile of v4, /device:TPU:16, one launch (start us, length us, event | category | flops | bytes accessed | tf_op | source)
XLA Modules:
  0.0 48.5 jit_solution(14186571573349281204)
XLA Ops:
  0.0 46.8 %shard_map.73 = bf16[256,512]{1,0:T(8,128)(2,1)} custom-call(bf16[3,256,256]{2,1,0:T(8,128)(2,1)} %bitcast.4, s32[1,256]{1,0:T(1,128)} %bitcast.5, s32[1,256]{1,0:T(1,128)} %bitcast.6, s32[1,256]{1,0:T(1,128)} %bitcast.7, bf16[256,2,16,256]{3,2,1,0:T(8,128)(2,1)} %kv_hbm.1, bf16[256,4096]{1,0:T(8,128)(2,1)} %w_hbm.1, bf16[256,512]{1,0:T(8,128)(2,1)} %res_hbm.1), custom_call_target="tpu_custom_call" | custom-call | tf_op jit(solution)/shard_map/pallas_call | solution.py:354
  46.8 1.7 %copy.9 = bf16[256,512]{1,0:T(8,128)(2,1)} copy(bf16[256,512]{1,0:T(8,128)(2,1)} %shard_map.73) | data formatting | bytes 524288

commit v5 on v4

--- a/solution.py
+++ b/solution.py
@@ -22,7 +22,7 @@
     fresh_hbm, act_hbm, home_hbm, len_hbm, kv_hbm, w_hbm, res_hbm,
     out_ref,
     fresh, small, kv, wcol, res, send, recv, rsend, rrecv,
-    gath, place, match, owned, score, att, own_sc, live, of_owner, of_row, acc, done,
+    gath, place, match, owned, score, att, own_sc, live, of_owner, of_row, acc,
     lsem, dat_ss, dat_rs, ret_ss, ret_rs, w_sem, wy_r, wm_r, ag_s, ag_r,
 ):
     n = small.shape[2]
@@ -331,8 +331,7 @@
         if m[0] == last:
             ring_copy(*m).wait_recv()
             rows = pl.ds(m[1] * hr, hr)
-            done[rows] = (acc[rows] + dot(gath[farthest, rows], wcol[order.index(ring // 2)])).astype(BF16)
-            pltpu.make_async_copy(done.at[rows], out_ref.at[rows], lsem.at[7]).start()
+            out_ref[rows] = (acc[rows] + dot(gath[farthest, rows], wcol[order.index(ring // 2)])).astype(BF16)
 
     for ex in (dat_x, ret_x):
         whole(*ex).wait_send()
@@ -340,7 +339,6 @@
     ring_all = gath.at[pl.ds(0, ring - 1)]
     pltpu.make_async_remote_copy(
         ring_all, ring_all, ag_s, ag_r.at[0], device_id={"tensor": y_peer(1)}, device_id_type=MESH).wait_send()
-    pltpu.make_async_copy(done, out_ref, lsem.at[7]).wait()
 
 
 def body(groups, ring, residual, fresh_qkv, active, home_slot, kv_cache, lengths, w_out):
@@ -353,9 +351,9 @@
     dma = pltpu.SemaphoreType.DMA
     return pl.pallas_call(
         functools.partial(kernel, groups, ring),
-        out_shape=jax.ShapeDtypeStruct((n, cols), BF16),
+        out_shape=pltpu.VMEM((n, cols), BF16),
         in_specs=[hbm] * 7,
-        out_specs=hbm,
+        out_specs=pl.BlockSpec(memory_space=pltpu.VMEM),
         scratch_shapes=[
             pltpu.VMEM((3, n, width), BF16),
             pltpu.VMEM((3, 1, n), I32),
@@ -377,8 +375,7 @@
             pltpu.VMEM((n, HD), BF16),
             pltpu.VMEM((2, n, HD), F32),
             pltpu.VMEM((n, cols), F32),
-            pltpu.VMEM((n, cols), BF16),
-            dma((8,)),
+            dma((7,)),
             dma, dma, dma, dma,
             dma, dma((2,)), dma((7,)), dma, dma((32,)),
         ],

time: 48.7 us -> 47 us (0.965)
  local copies, waits for them, and re-layouts: 1.67 us -> 0.71 us
  Pallas kernels: 46.8 us -> 46.2 us
    unnamed x1, local copies, waits for them, and re-layouts: 1.67 us -> 0.71 us
    pallas_call x1, Pallas kernels: 46.8 us -> 46.2 us  [body(): pl.pallas_call(functools.partial(kernel, groups, ring), out_shape=pltpu.V...]
where the time goes in v5:
time: 47 us; the launch traced here: 46.9 us
  Pallas kernels  46.2 us (98%)
  local copies, waits for them, and re-layouts  0.71 us (2%)
    pallas_call x1, Pallas kernels, body(): pl.pallas_call(functools.partial(kernel, groups, ring), out_shape=pltpu.V...  46.2 us

profile of v5, /device:TPU:16, one launch (start us, length us, event | category | flops | bytes accessed | tf_op | source)
XLA Modules:
  0.0 46.9 jit_solution(3080041043484206114)
XLA Ops:
  0.0 46.2 %shard_map.73 = bf16[256,512]{1,0:T(8,128)(2,1)S(1)} custom-call(bf16[3,256,256]{2,1,0:T(8,128)(2,1)} %bitcast.4, s32[1,256]{1,0:T(1,128)} %bitcast.5, s32[1,256]{1,0:T(1,128)} %bitcast.6, s32[1,256]{1,0:T(1,128)} %bitcast.7, bf16[256,2,16,256]{3,2,1,0:T(8,128)(2,1)} %kv_hbm.1, bf16[256,4096]{1,0:T(8,128)(2,1)} %w_hbm.1, bf16[256,512]{1,0:T(8,128)(2,1)} %res_hbm.1), custom_call_target="tpu_custom_call" | custom-call | tf_op jit(solution)/shard_map/pallas_call | solution.py:352
  46.2 0.7 %copy.9 = bf16[256,512]{1,0:T(8,128)(2,1)} copy(bf16[256,512]{1,0:T(8,128)(2,1)S(1)} %shard_map.73) | data formatting | bytes 524288

commit v6 on v5

--- a/solution.py
+++ b/solution.py
@@ -22,7 +22,7 @@
     fresh_hbm, act_hbm, home_hbm, len_hbm, kv_hbm, w_hbm, res_hbm,
     out_ref,
     fresh, small, kv, wcol, res, send, recv, rsend, rrecv,
-    gath, place, match, owned, score, att, own_sc, live, of_owner, of_row, acc,
+    gath, place, match, owned, score, att, own_sc, live, of_owner, of_row, bias, acc,
     lsem, dat_ss, dat_rs, ret_ss, ret_rs, w_sem, wy_r, wm_r, ag_s, ag_r,
 ):
     n = small.shape[2]
@@ -175,7 +175,12 @@
     def as_column(row, wide):
         return dot(jnp.where(eye, row, 0).astype(BF16), jnp.ones((n, wide), BF16))
 
+    blocks = n // 16
+    lane_i = lax.broadcasted_iota(I32, (n, 16 * length), 1)
+    row_i = lax.broadcasted_iota(I32, (n, 16 * length), 0)
     lengths = as_column(small[2].astype(F32), 16 * length)
+    valid = (lane_i // length == row_i % 16) & ((lane_i % length).astype(F32) < lengths)
+    bias[...] = jnp.where(valid, 0.0, -1e30)
     owner_col = as_column(jnp.where(active, owner, -8).astype(F32), groups * 8)
     rank_col = as_column(rank, groups * 8)
     spot_col = (owner_col * 8 + rank_col).astype(I32)
@@ -206,10 +211,6 @@
         owned[h] = dot(match[h], arrived).astype(BF16)
 
     kv_cp.wait()
-    blocks = n // 16
-    lane_i = lax.broadcasted_iota(I32, (n, 16 * length), 1)
-    row_i = lax.broadcasted_iota(I32, (n, 16 * length), 0)
-    valid = (lane_i // length == row_i % 16) & ((lane_i % length).astype(F32) < lengths)
     none = jnp.zeros((16, HD), BF16)
     for i in range(blocks):
         rows = slice(16 * i, 16 * i + 16)
@@ -218,36 +219,29 @@
         both = dot(query, kv[rows, 0].reshape(16 * length, 2 * HD), 1, 1)
         score[0, rows] = both[0:16]
         score[1, rows] = both[16:32]
-    lse_of, weights = [], []
+    weights, terms = [], []
     for h in range(2):
-        s = jnp.where(valid, score[h] * scale, -1e30)
+        s = score[h] * scale + bias[...]
         top = jnp.max(s, axis=1, keepdims=True)
-        e = jnp.where(valid, jnp.exp(s - top), 0.0)
+        e = jnp.exp(s - top)
         total = jnp.sum(e, axis=1, keepdims=True)
         weights.append((e * (1.0 / total)).astype(BF16))
-        lse_of.append(top + jnp.log(total))
+        lse = jnp.broadcast_to(top + jnp.log(total), (n, HD))
+        high = lse.astype(BF16).astype(F32)
+        middle = (lse - high).astype(BF16).astype(F32)
+        low = lse - high - middle
+        terms.append(jnp.where(
+            lane_n < 8, high, jnp.where(lane_n < 16, middle, jnp.where(lane_n < 24, low, 0.0))).astype(BF16))
     for i in range(blocks):
         rows = slice(16 * i, 16 * i + 16)
         both = dot(jnp.concatenate([weights[0][rows], weights[1][rows]], axis=0), kv[rows, 1].reshape(16 * length, 2 * HD))
         att[0, rows] = both[0:16, 0:HD].astype(BF16)
         att[1, rows] = both[16:32, HD:2 * HD].astype(BF16)
-    lse_row = jnp.sum(
-        match[0].astype(F32) * lse_of[0] + match[1].astype(F32) * lse_of[1], axis=0, keepdims=True)
-    back = dot(match[0], att[0], 0, 0) + dot(match[1], att[1], 0, 0)
-    rsend[:, 0:4] = back.astype(BF16).reshape(groups, 4, 2, HD)
-    spread = jnp.zeros((groups, 128), F32)
-    group_i = lax.broadcasted_iota(I32, (groups, 128), 0)
-    for b in range(groups // 16):
-        spread = jnp.where(group_i // 16 == b, lse_row[:, b * 128:(b + 1) * 128], spread)
-    lse_rows = jnp.zeros((groups, 128), F32)
-    for i in range(8):
-        value = jnp.sum(jnp.where(lane == (group_i % 16) * 8 + i, spread, 0.0), axis=1, keepdims=True)
-        lse_rows = jnp.where(lane % 8 == i, value, lse_rows)
-    high = lse_rows.astype(BF16).astype(F32)
-    middle = (lse_rows - high).astype(BF16).astype(F32)
-    low = lse_rows - high - middle
-    terms = jnp.where(lane < 8, high, jnp.where(lane < 16, middle, jnp.where(lane < 24, low, 0.0)))
-    rsend[:, 4] = fifth(terms)
+    back = sum(
+        dot(match[h], jnp.concatenate([att[h], terms[h]], axis=1), 0, 0) for h in range(2))
+    rsend[:, 0:4] = back[:, 0:HD].astype(BF16).reshape(groups, 4, 2, HD)
+    one_lane = lax.broadcasted_iota(I32, (groups * 8, HD), 1) % 8 == lax.broadcasted_iota(I32, (groups * 8, HD), 0) % 8
+    rsend[:, 4] = fifth(jnp.sum(jnp.where(one_lane, back[:, HD:], 0.0).reshape(groups, 8, HD), axis=1))
 
     each_peer(lambda to: to_peer(*ret_x, to).start())
     keep[1].start()
@@ -264,7 +258,7 @@
         src = lax.rem(y + (ring - s if way > 0 else s), ring)
         to = lax.rem(y + (1 if way > 0 else ring - 1), ring)
         at = gath.at[src, pl.ds(q * hr, hr)]
-        i = (s * pieces + q) * 2 + (way > 0)
+        i = moves.index((s, q, way))
         return pltpu.make_async_remote_copy(
             at, at, ag_s, ag_r.at[i], device_id={"tensor": to}, device_id_type=MESH)
 
@@ -374,10 +368,11 @@
             pltpu.VMEM((n, HD), F32),
             pltpu.VMEM((n, HD), BF16),
             pltpu.VMEM((2, n, HD), F32),
+            pltpu.VMEM((n, 16 * length), F32),
             pltpu.VMEM((n, cols), F32),
             dma((7,)),
             dma, dma, dma, dma,
-            dma, dma((2,)), dma((7,)), dma, dma((32,)),
+            dma, dma((2,)), dma((7,)), dma, dma((28,)),
         ],
         compiler_params=pltpu.CompilerParams(collective_id=0, has_side_effects=True),
     )(

time: 47 us -> 47 us (level)
  no operation moved by 1% of the time
where the time goes in v6:
time: 47 us; the launch traced here: 46.8 us
  Pallas kernels  46.1 us (98%)
  local copies, waits for them, and re-layouts  0.71 us (2%)
    pallas_call x1, Pallas kernels, body(): pl.pallas_call(functools.partial(kernel, groups, ring), out_shape=pltpu.V...  46.1 us

profile of v6, /device:TPU:16, one launch (start us, length us, event | category | flops | bytes accessed | tf_op | source)
XLA Modules:
  0.0 46.8 jit_solution(4714341784484601217)
XLA Ops:
  0.0 46.1 %shard_map.73 = bf16[256,512]{1,0:T(8,128)(2,1)S(1)} custom-call(bf16[3,256,256]{2,1,0:T(8,128)(2,1)} %bitcast.4, s32[1,256]{1,0:T(1,128)} %bitcast.5, s32[1,256]{1,0:T(1,128)} %bitcast.6, s32[1,256]{1,0:T(1,128)} %bitcast.7, bf16[256,2,16,256]{3,2,1,0:T(8,128)(2,1)} %kv_hbm.1, bf16[256,4096]{1,0:T(8,128)(2,1)} %w_hbm.1, bf16[256,512]{1,0:T(8,128)(2,1)} %res_hbm.1), custom_call_target="tpu_custom_call" | custom-call | tf_op jit(solution)/shard_map/pallas_call | solution.py:346
  46.1 0.7 %copy.9 = bf16[256,512]{1,0:T(8,128)(2,1)} copy(bf16[256,512]{1,0:T(8,128)(2,1)S(1)} %shard_map.73) | data formatting | bytes 524288
